TPU v7x, 256 devices: a whole 4x4x8 slice. The times are simulated.
256 devices in a mesh: dp: 64 (over x, z, y_hi), mp: 4 (over y_lo, core).
Axes of the slice: x: 4, y: 4 (y_hi: 2, y_lo: 2; y = y_hi * 2 + y_lo), z: 8, core: 2. Of those that a mesh axis runs over, the one named last changes fastest.
Arguments:
- media: bfloat16 [128, 8, 256, 1024], P('dp'), may hold values from -6 to 6
- latents: bfloat16 [64, 1024], replicated, may hold values from -6 to 6
- time_embed: bfloat16 [8, 1024], replicated, may hold values from -5 to 5
- media_gain: float32 [2, 1024], replicated, may hold values from 0.25 to 1.75
- latent_gain: float32 [2, 1024], replicated, may hold values from 0.25 to 1.75
- ffn_gain: float32 [2, 1024], replicated, may hold values from 0.25 to 1.75
- out_gain: float32 [1024], replicated, may hold values from 0.25 to 1.75
- w_query: bfloat16 [2, 1024, 512], P(None, 'dp', 'mp'), may hold values from -0.1875 to 0.1875
- w_key: bfloat16 [2, 1024, 512], P(None, 'dp', 'mp'), may hold values from -0.1875 to 0.1875
- w_value: bfloat16 [2, 1024, 512], P(None, 'dp', 'mp'), may hold values from -0.1875 to 0.1875
- w_out: bfloat16 [2, 512, 1024], P(None, 'mp', 'dp'), may hold values from -0.25 to 0.25
- w_up: bfloat16 [2, 1024, 4096], P(None, 'dp', 'mp'), may hold values from -0.1875 to 0.1875
- w_down: bfloat16 [2, 4096, 1024], P(None, 'mp', 'dp'), may hold values from -0.09375 to 0.09375
Outputs:
- resampled: bfloat16 [128, 64, 1024], P('dp')
All inputs are finite; a program needn't handle non-finite values.
Results may differ from a plain program's by a relative error of at most 0.013.
Values may be sent and summed in bfloat16 or wider, within the bound.
No kernel may reach another device: no remote copies, remote signals or barrier semaphores. Data moves between devices by JAX's collectives and lax.ppermute only.
A program may use at most 128 MiB of HBM per device.

v0:
```python
import jax
import jax.numpy as jnp
from jax import lax
from jax.sharding import PartitionSpec as P

HEAD = 64
LAYERS = 2


def in_one_piece(arrays, axis, dim, along):
    widths = [a.shape[along] for a in arrays]
    both = jnp.concatenate(arrays, axis=along)
    filled = lax.all_gather(both, axis, axis=dim, tiled=True)
    return tuple(jnp.split(filled, [sum(widths[:k]) for k in range(1, len(widths))], axis=along))


def copy_for_each(x, axis):
    copies = jnp.broadcast_to(x, (lax.axis_size(axis), *x.shape))
    return lax.all_to_all(copies, axis, split_axis=0, concat_axis=0, tiled=True)


def of_everyone(x, axis):
    everything = copy_for_each(x, axis)
    return jnp.sum(everything.astype(jnp.float32), axis=0)


def layer_norm(values, gain):
    center = values - jnp.mean(values, axis=-1, keepdims=True)
    spread = jnp.mean(center * center, axis=-1, keepdims=True)
    return center * lax.rsqrt(spread + 1e-05) * gain


def matmul(left, right):
    return jnp.dot(left, right, preferred_element_type=jnp.float32)


def on_device(
    media,
    latents,
    time_embed,
    media_gain,
    latent_gain,
    ffn_gain,
    out_gain,
    w_query,
    w_key,
    w_value,
    w_out,
    w_up,
    w_down,
):
    samples = media.shape[0]
    frames = media.shape[1]
    patches = media.shape[2]
    width = media.shape[3]
    count = latents.shape[0]
    head_size = HEAD
    local_heads = w_query.shape[2] // head_size
    scale = head_size ** (-0.5)
    tokens = frames * patches
    flat = (media.astype(jnp.float32) + time_embed.astype(jnp.float32)[None, :, None, :]).reshape(
        samples * tokens, width
    )
    state = jnp.broadcast_to(latents.astype(jnp.float32)[None], (samples, count, width)).reshape(
        samples * count, width
    )
    row_parts = in_one_piece((w_query, w_key, w_value, w_up), "dp", 1, 2)
    col_parts = (
        lax.all_gather(w_out, "dp", axis=2, tiled=True),
        lax.all_gather(w_down, "dp", axis=2, tiled=True),
    )

    def full_rows(values, gain):
        normed = layer_norm(values, gain).astype(jnp.bfloat16)
        return normed

    def add_update(current, partial_value):
        return current + of_everyone(partial_value.astype(jnp.bfloat16), "mp").astype(jnp.float32)

    for layer in range(LAYERS):
        query_weight = row_parts[0][layer]
        key_weight = row_parts[1][layer]
        value_weight = row_parts[2][layer]
        up_weight = row_parts[3][layer]
        out_weight = col_parts[0][layer]
        down_weight = col_parts[1][layer]
        media_normed = layer_norm(flat, media_gain[layer]).astype(jnp.bfloat16)
        latent_normed = full_rows(state, latent_gain[layer])
        query = matmul(latent_normed, query_weight)
        key_media = matmul(media_normed, key_weight)
        value_media = matmul(media_normed, value_weight)
        key_latent = matmul(latent_normed, key_weight)
        value_latent = matmul(latent_normed, value_weight)
        queries = (
            (query * scale).astype(jnp.bfloat16).reshape(samples, count, local_heads, head_size)
        )
        keys = jnp.concatenate(
            [
                key_media.astype(jnp.bfloat16).reshape(samples, tokens, local_heads, head_size),
                key_latent.astype(jnp.bfloat16).reshape(samples, count, local_heads, head_size),
            ],
            axis=1,
        )
        values = jnp.concatenate(
            [
                value_media.astype(jnp.bfloat16).reshape(samples, tokens, local_heads, head_size),
                value_latent.astype(jnp.bfloat16).reshape(samples, count, local_heads, head_size),
            ],
            axis=1,
        )
        scores = jnp.einsum("sqhd,skhd->shqk", queries, keys, preferred_element_type=jnp.float32)
        probs = jax.nn.softmax(scores, axis=-1).astype(jnp.bfloat16)
        attended = jnp.einsum("shqk,skhd->sqhd", probs, values, preferred_element_type=jnp.float32)
        attended = attended.astype(jnp.bfloat16).reshape(samples * count, local_heads * head_size)
        state = add_update(state, matmul(attended, out_weight))
        ffn_normed = full_rows(state, ffn_gain[layer])
        hidden = jax.nn.gelu(matmul(ffn_normed, up_weight), approximate=False).astype(jnp.bfloat16)
        state = add_update(state, matmul(hidden, down_weight))
    final = layer_norm(state, out_gain).astype(jnp.bfloat16)
    return final.reshape(samples, count, width)


def solution(mesh):
    in_specs = (
        P("dp", None, None, None),
        P(),
        P(),
        P(),
        P(),
        P(),
        P(),
        P(None, "dp", "mp"),
        P(None, "dp", "mp"),
        P(None, "dp", "mp"),
        P(None, "mp", "dp"),
        P(None, "dp", "mp"),
        P(None, "mp", "dp"),
    )
    out_specs = P("dp", None, None)
    return jax.shard_map(
        on_device, mesh=mesh, in_specs=in_specs, out_specs=out_specs, check_vma=False
    )
```

profile of v0, /device:TPU:32, one launch (start us, length us, event | category | flops | bytes accessed | tf_op | source)
XLA Modules:
  0.0 386.2 jit_solution(2744716518895289468)
XLA Ops:
  6.5 1.5 pad_maximum_fusion
  13.3 5.3 %fusion.3 = f32[2,8,256]{2,1,0:T(8,128)S(1)} fusion(bf16[2,8,256,1024]{3,2,1,0:T(8,128)(2,1)} %param.13, f32[8,1024]{1,0:T(8,128)S(1)} %convert_element_type.171), kind=kLoop, calls=%fused_computation.7 | loop fusion | flops 12578816 | bytes 8437760 | tf_op jit(solution)/shard_map/reduce_sum | solution.py:28
  19.1 3.2 multiply_reduce_fusion
  22.4 183.6 %all_gather.10 = bf16[2,128,1024]{1,2,0:T(8,128)(2,1)S(1)} all-gather(bf16[2,128,16]{1,2,0:T(8,128)(2,1)S(1)} %copy-done.1), channel_id=1, replica_groups=mesh['dp'=64,'mp'=4] {'dp'}, dimensions={2}, use_global_device_ids=true | all-gather | bytes 532480 | tf_op jit(solution)/shard_map/all_gather | solution.py:69
  206.1 7.3 %multiply_convert_fusion = (bf16[2,8,256,1024]{3,2,1,0:T(8,128)(2,1)}, bf16[2,8,256,1024]{3,2,1,0:T(8,128)(2,1)}) fusion(bf16[2,8,256,1024]{3,2,1,0:T(8,128)(2,1)S(1)} %copy-done, f32[1024]{0:T(1024)S(1)} %bitcast.118, f32[2,8,256]{2,1,0:T(8,128)S(1)} %add_rsqrt_fusion, f32[2,8,256]{2,1,0:T(8,128)S(1)} %broadcast_multiply_fusion, ...), kind=kLoop, calls=%fused_computation.2 | loop fusion | flops 33554432 | bytes 25239552 | tf_op jit(solution)/shard_map/convert_element_type | solution.py:87
  213.3 1.2 convolution_convert_fusion.10
  216.0 6.8 %convolution_convert_fusion.2 = bf16[4096,128]{1,0:T(8,128)(2,1)} fusion(bf16[4096,1024]{1,0:T(8,128)(2,1)} %bitcast.100, bf16[2,1024,1408]{2,1,0:T(8,128)(2,1)} %all-gather.3.cloned.1.call-done), kind=kOutput, calls=%fused_computation.11 | convolution fusion | flops 1074266112 | bytes 9699328 | tf_op jit(solution)/shard_map/dot_general | solution.py:34
  222.7 3.9 %reshape.1012 = bf16[2,2048,2,64]{3,2,1,0:T(2,128)(2,1)S(1)} reshape(bf16[4096,128]{1,0:T(8,128)(2,1)} %convolution_convert_fusion.2) | data formatting | bytes 2097152 | tf_op jit(solution)/shard_map/reshape | solution.py:99
  226.6 3.6 copy.44
  231.5 6.7 %convolution_convert_fusion.3 = bf16[4096,128]{1,0:T(8,128)(2,1)} fusion(bf16[4096,1024]{1,0:T(8,128)(2,1)} %bitcast.101, bf16[2,1024,1408]{2,1,0:T(8,128)(2,1)} %all-gather.3.cloned.1.call-done), kind=kOutput, calls=%fused_computation.12 | convolution fusion | flops 1074266112 | bytes 9699328 | tf_op jit(solution)/shard_map/dot_general | solution.py:34
  238.3 3.9 %reshape.1011 = bf16[2,2048,2,64]{3,2,1,0:T(2,128)(2,1)S(1)} reshape(bf16[4096,128]{1,0:T(8,128)(2,1)} %convolution_convert_fusion.3) | data formatting | bytes 2097152 | tf_op jit(solution)/shard_map/reshape | solution.py:106
  242.1 3.5 copy.41
  245.6 3.3 fusion.215
  248.9 2.5 fusion.15
  251.9 1.2 broadcast_in_dim.13
  253.1 3.7 all-to-all-start
  256.9 14.2 %all-to-all-done = bf16[4,128,1024]{2,1,0:T(8,128)(2,1)S(1)} async-done(((bf16[4,128,1024]{2,1,0:T(8,128)(2,1)}), bf16[4,128,1024]{2,1,0:T(8,128)(2,1)S(1)}, u32[]{:S(2)}, u32[]{:S(2)}) %all-to-all-start) | async-done | bytes 1048608 | tf_op jit(solution)/shard_map/all_to_all | solution.py:19
  271.9 15.6 %all-gather.5.cloned.1.call-done = bf16[2,1024,1024]{1,2,0:T(8,128)(2,1)} async-done(((bf16[2,1024,16]{1,2,0:T(8,128)(2,1)}), bf16[2,1024,1024]{1,2,0:T(8,128)(2,1)}) %all-gather.5.cloned.1.call-update) | async-done | bytes 4194320 | tf_op jit(solution)/shard_map/all_gather | solution.py:70
  287.5 4.4 %fusion.13 = bf16[128,1024]{1,0:T(8,128)(2,1)S(1)} fusion(bf16[2,1024,1024]{1,2,0:T(8,128)(2,1)} %all-gather.5.cloned.1.call-done, bf16[128,1024]{1,0:T(8,128)(2,1)S(1)} %bitcast.113, bf16[2,1024,1408]{2,1,0:T(8,128)(2,1)} %all-gather.3.cloned.1.call-done), kind=kOutput, calls=%fused_computation.31 | convolution fusion | flops 545521664 | bytes 4718592 | tf_op jit(solution)/shard_map/dot_general | solution.py:34
  293.0 4.2 %all-to-all-start.1 = ((bf16[4,128,1024]{2,1,0:T(8,128)(2,1)}), bf16[4,128,1024]{2,1,0:T(8,128)(2,1)}, u32[]{:S(2)}, u32[]{:S(2)}) async-start(bf16[4,128,1024]{2,1,0:T(8,128)(2,1)} %broadcast_in_dim.15), calls=%async_computation.1 | async-start | bytes 2097152 | tf_op jit(solution)/shard_map/all_to_all | solution.py:19
  297.2 6.7 %convolution_convert_fusion = bf16[4096,128]{1,0:T(8,128)(2,1)} fusion(bf16[4096,1024]{1,0:T(8,128)(2,1)} %bitcast.98, bf16[2,1024,1408]{2,1,0:T(8,128)(2,1)} %all-gather.3.cloned.1.call-done), kind=kOutput, calls=%fused_computation.9 | convolution fusion | flops 1074266112 | bytes 9699328 | tf_op jit(solution)/shard_map/dot_general | solution.py:34
  304.0 3.9 %reshape.1014 = bf16[2,2048,2,64]{3,2,1,0:T(2,128)(2,1)S(1)} reshape(bf16[4096,128]{1,0:T(8,128)(2,1)} %convolution_convert_fusion) | data formatting | bytes 2097152 | tf_op jit(solution)/shard_map/reshape | solution.py:99
  307.8 3.6 copy.52
  311.4 6.7 %convolution_convert_fusion.1 = bf16[4096,128]{1,0:T(8,128)(2,1)} fusion(bf16[4096,1024]{1,0:T(8,128)(2,1)} %bitcast.99, bf16[2,1024,1408]{2,1,0:T(8,128)(2,1)} %all-gather.3.cloned.1.call-done), kind=kOutput, calls=%fused_computation.10 | convolution fusion | flops 1074266112 | bytes 9699328 | tf_op jit(solution)/shard_map/dot_general | solution.py:34
  318.1 3.9 %reshape.1013 = bf16[2,2048,2,64]{3,2,1,0:T(2,128)(2,1)S(1)} reshape(bf16[4096,128]{1,0:T(8,128)(2,1)} %convolution_convert_fusion.1) | data formatting | bytes 2097152 | tf_op jit(solution)/shard_map/reshape | solution.py:106
  322.0 3.6 copy.49
  325.5 1.5 convert_reduce_fusion.2
  331.7 3.2 fusion.220
  335.0 2.5 fusion.16
  338.0 17.5 %all_to_all.20 = bf16[4,128,1024]{2,1,0:T(8,128)(2,1)S(1)} all-to-all(bf16[4,128,1024]{2,1,0:T(8,128)(2,1)S(1)} %broadcast_in_dim.16), channel_id=1, replica_groups=mesh['dp'=64,'mp'=4] {'mp'}, dimensions={0} | all-to-all | bytes 2097152 | tf_op jit(solution)/shard_map/all_to_all | solution.py:19
  356.4 4.4 %fusion.14 = bf16[128,1024]{1,0:T(8,128)(2,1)S(1)} fusion(bf16[2,1024,1024]{1,2,0:T(8,128)(2,1)} %all-gather.5.cloned.1.call-done, bf16[128,1024]{1,0:T(8,128)(2,1)S(1)} %bitcast.112, bf16[2,1024,1408]{2,1,0:T(8,128)(2,1)} %all-gather.3.cloned.1.call-done), kind=kOutput, calls=%fused_computation.32 | convolution fusion | flops 545521664 | bytes 4718592 | tf_op jit(solution)/shard_map/dot_general | solution.py:34
  361.0 16.9 %all_to_all.21 = bf16[4,128,1024]{2,1,0:T(8,128)(2,1)S(1)} all-to-all(bf16[4,128,1024]{2,1,0:T(8,128)(2,1)S(1)} %broadcast_in_dim.17), channel_id=1, replica_groups=mesh['dp'=64,'mp'=4] {'mp'}, dimensions={0} | all-to-all | bytes 2097152 | tf_op jit(solution)/shard_map/all_to_all | solution.py:19
  (81 shorter events, 18.8 us)
Async XLA Ops:
  6.5 206.8 %all-gather.3.cloned.1.call-start = ((), (), s32[]{:S(2)}) async-start(), calls=%async_computation.4 | async-start | bytes 5857280 | tf_op jit(solution)/shard_map/all_gather | solution.py:13
  8.1 279.4 %all-gather.5.cloned.1.call-start = ((), (), s32[]{:S(2)}) async-start(), calls=%async_computation.5 | async-start | bytes 4259840 | tf_op jit(solution)/shard_map/all_gather | solution.py:70
  13.3 5.8 %copy-start = (bf16[2,8,256,1024]{3,2,1,0:T(8,128)(2,1)S(1)}, bf16[2,8,256,1024]{3,2,1,0:T(8,128)(2,1)}, u32[]{:S(2)}) copy-start(bf16[2,8,256,1024]{3,2,1,0:T(8,128)(2,1)} %param.13) | copy-start | bytes 25165828
  19.0 3.4 copy-start.1
  251.5 5.4 %copy-start.2 = (f32[2,1024]{1,0:T(2,128)S(1)}, f32[2,1024]{1,0:T(2,128)}, u32[]{:S(2)}) copy-start(f32[2,1024]{1,0:T(2,128)} %param.18) | copy-start | bytes 24580
  253.1 17.9 %all-to-all-start = ((bf16[4,128,1024]{2,1,0:T(8,128)(2,1)}), bf16[4,128,1024]{2,1,0:T(8,128)(2,1)S(1)}, u32[]{:S(2)}, u32[]{:S(2)}) async-start(bf16[4,128,1024]{2,1,0:T(8,128)(2,1)} %broadcast_in_dim.13), calls=%async_computation | async-start | bytes 2097152 | tf_op jit(solution)/shard_map/all_to_all | solution.py:19
  293.0 32.6 %all-to-all-start.1 = ((bf16[4,128,1024]{2,1,0:T(8,128)(2,1)}), bf16[4,128,1024]{2,1,0:T(8,128)(2,1)}, u32[]{:S(2)}, u32[]{:S(2)}) async-start(bf16[4,128,1024]{2,1,0:T(8,128)(2,1)} %broadcast_in_dim.15), calls=%async_computation.1 | async-start | bytes 2097152 | tf_op jit(solution)/shard_map/all_to_all | solution.py:19
  360.8 17.7 %copy-start.3 = (f32[1024]{0:T(1024)S(1)}, f32[1024]{0:T(1024)}, u32[]{:S(2)}) copy-start(f32[1024]{0:T(1024)} %param.19) | copy-start | bytes 12292
Sparse Core Ops, SparseCore 0:
  11.0 137.5 all-gather.2
  152.1 135.3 all-gather.4
where the time goes:
time: 387 us; the launch traced here: 386 us
  blocking collectives  218 us (56%)
  matrix products  54.6 us (14%)
  local copies, waits for them, and re-layouts  36.3 us (9%)
  waiting for transfers between devices  30.4 us (8%)
  other arithmetic  25 us (6%)
  between operations  13.8 us (4%)
  starting transfers between devices  8.04 us (2%)
    all_gather x1, blocking collectives, on_device(): lax.all_gather(w_out, 'dp', axis=2, tiled=True)  184 us
    dot_general x14, matrix products, matmul(): return jnp.dot(left, right, preferred_element_type=jnp.float32)  43.1 us
    all_to_all x2, blocking collectives, copy_for_each(): return lax.all_to_all(copies, axis, split_axis=0, concat_axis=0, tiled=True)  34.3 us
    all_gather x1, waiting for transfers between devices, on_device(): lax.all_gather(w_down, 'dp', axis=2, tiled=True)  15.6 us
    reshape x4, local copies, waits for them, and re-layouts, on_device(): key_media.astype(jnp.bfloat16)  14.9 us
    reshape x4, local copies, waits for them, and re-layouts, on_device(): value_media.astype(jnp.bfloat16)  14.8 us
    all_to_all x2, waiting for transfers between devices, copy_for_each(): return lax.all_to_all(copies, axis, split_axis=0, concat_axis=0, tiled=True)  14.2 us
    all_to_all x2, starting transfers between devices, copy_for_each(): return lax.all_to_all(copies, axis, split_axis=0, concat_axis=0, tiled=True)  8 us
  transfers between devices with their start and end apart: 4, of which 2 were waited for; matrix products, arithmetic and copies ran while one was open for 23% of the time, Pallas kernels for 0%

commit v1 on v0

--- a/solution.py
+++ b/solution.py
@@ -5,6 +5,13 @@
 
 HEAD = 64
 LAYERS = 2
+
+
+def exchange_gather(x, name, dim):
+    size = lax.axis_size(name)
+    parts = jnp.stack([x for _ in range(size)])
+    parts = lax.all_to_all(parts, name, split_axis=0, concat_axis=0)
+    return jnp.concatenate(parts, axis=dim)
 
 
 def in_one_piece(arrays, axis, dim, along):
@@ -65,10 +72,7 @@
         samples * count, width
     )
     row_parts = in_one_piece((w_query, w_key, w_value, w_up), "dp", 1, 2)
-    col_parts = (
-        lax.all_gather(w_out, "dp", axis=2, tiled=True),
-        lax.all_gather(w_down, "dp", axis=2, tiled=True),
-    )
+    col_parts = (exchange_gather(w_out, "dp", 2), lax.all_gather(w_down, "dp", axis=2, tiled=True))
 
     def full_rows(values, gain):
         normed = layer_norm(values, gain).astype(jnp.bfloat16)

time: 387 us -> 375 us (0.969)
  blocking collectives: 218 us -> 34.3 us
  waiting for transfers between devices: 30.4 us -> 185 us
  starting transfers between devices: 8.04 us -> 22.2 us
    all_gather x1 -> x0, blocking collectives: 184 us -> none  [on_device(): lax.all_gather(w_out, 'dp', axis=2, tiled=True)]
    all_gather x1, waiting for transfers between devices: 0.01 us -> 101 us  [in_one_piece(): filled = lax.all_gather(both, axis, axis=dim, tiled=True)]
    all_gather x1, waiting for transfers between devices: 15.6 us -> 67.2 us  [on_device(): lax.all_gather(w_down, 'dp', axis=2, tiled=True)]
    all_to_all x0 -> x1, starting transfers between devices: none -> 14.2 us  [exchange_gather(): parts = lax.all_to_all(parts, name, split_axis=0, concat_axis=0)]
  transfers between devices with their start and end apart: 4 -> 5, of which waited for: 2 -> 3; matrix products, arithmetic and copies ran while one was open for 23% -> 24% of each run, Pallas kernels for 0% -> 0%
where the time goes in v1:
time: 375 us; the launch traced here: 372 us
  waiting for transfers between devices  185 us (49%)
  matrix products  52.2 us (14%)
  local copies, waits for them, and re-layouts  39.5 us (11%)
  blocking collectives  34.3 us (9%)
  other arithmetic  25.1 us (7%)
  starting transfers between devices  22.2 us (6%)
  between operations  13.8 us (4%)
    all_gather x1, waiting for transfers between devices, in_one_piece(): filled = lax.all_gather(both, axis, axis=dim, tiled=True)  101 us
    all_gather x1, waiting for transfers between devices, on_device(): lax.all_gather(w_down, 'dp', axis=2, tiled=True)  67.2 us
    dot_general x14, matrix products, matmul(): return jnp.dot(left, right, preferred_element_type=jnp.float32)  43.1 us
    all_to_all x2, blocking collectives, copy_for_each(): return lax.all_to_all(copies, axis, split_axis=0, concat_axis=0, tiled=True)  34.3 us
    all_to_all x2, waiting for transfers between devices, copy_for_each(): return lax.all_to_all(copies, axis, split_axis=0, concat_axis=0, tiled=True)  16.1 us
    reshape x4, local copies, waits for them, and re-layouts, on_device(): value_media.astype(jnp.bfloat16)  14.9 us
    reshape x4, local copies, waits for them, and re-layouts, on_device(): key_media.astype(jnp.bfloat16)  14.9 us
    all_to_all x1, starting transfers between devices, exchange_gather(): parts = lax.all_to_all(parts, name, split_axis=0, concat_axis=0)  14.2 us
  transfers between devices with their start and end apart: 5, of which 3 were waited for; matrix products, arithmetic and copies ran while one was open for 24% of the time, Pallas kernels for 0%

profile of v1, /device:TPU:32, one launch (start us, length us, event | category | flops | bytes accessed | tf_op | source)
XLA Modules:
  0.0 372.3 jit_solution(3923963577337899368)
XLA Ops:
  6.5 1.5 pad_maximum_fusion
  8.1 1.6 stack.2
  9.6 14.2 %all-to-all-start = ((bf16[64,2,128,16]{2,3,1,0:T(8,128)(2,1)}), bf16[64,2,128,16]{2,3,1,0:T(8,128)(2,1)S(1)}, u32[]{:S(2)}, u32[]{:S(2)}) async-start(bf16[64,2,128,16]{2,3,1,0:T(8,128)(2,1)} %stack.2), calls=%async_computation | async-start | bytes 1048576 | tf_op jit(solution)/shard_map/all_to_all | solution.py:13
  29.1 5.3 %fusion.3 = f32[2,8,256]{2,1,0:T(8,128)S(1)} fusion(bf16[2,8,256,1024]{3,2,1,0:T(8,128)(2,1)} %param.13, f32[8,1024]{1,0:T(8,128)S(1)} %convert_element_type.171), kind=kLoop, calls=%fused_computation.7 | loop fusion | flops 12578816 | bytes 8437760 | tf_op jit(solution)/shard_map/reduce_sum | solution.py:35
  34.9 3.2 multiply_reduce_fusion
  38.2 7.3 %multiply_convert_fusion = (bf16[2,8,256,1024]{3,2,1,0:T(8,128)(2,1)}, bf16[2,8,256,1024]{3,2,1,0:T(8,128)(2,1)}) fusion(bf16[2,8,256,1024]{3,2,1,0:T(8,128)(2,1)S(1)} %copy-done, f32[1024]{0:T(1024)S(1)} %bitcast.122, f32[2,8,256]{2,1,0:T(8,128)S(1)} %add_rsqrt_fusion, f32[2,8,256]{2,1,0:T(8,128)S(1)} %broadcast_multiply_fusion, ...), kind=kLoop, calls=%fused_computation.2 | loop fusion | flops 33554432 | bytes 25239552 | tf_op jit(solution)/shard_map/convert_element_type | solution.py:91
  46.4 101.1 %all-gather.3.cloned.1.call-done = bf16[2,1024,1408]{2,1,0:T(8,128)(2,1)} async-done(((bf16[2,16,1408]{2,1,0:T(8,128)(2,1)}), bf16[2,1024,1408]{2,1,0:T(8,128)(2,1)}) %all-gather.3.cloned.1.call-update) | async-done | bytes 5767184 | tf_op jit(solution)/shard_map/all_gather | solution.py:20
  150.1 6.7 %convolution_convert_fusion.2 = bf16[4096,128]{1,0:T(8,128)(2,1)} fusion(bf16[4096,1024]{1,0:T(8,128)(2,1)} %bitcast.101, bf16[2,1024,1408]{2,1,0:T(8,128)(2,1)} %all-gather.3.cloned.1.call-done), kind=kOutput, calls=%fused_computation.11 | convolution fusion | flops 1074266112 | bytes 9699328 | tf_op jit(solution)/shard_map/dot_general | solution.py:41
  156.8 3.9 %reshape.1023 = bf16[2,2048,2,64]{3,2,1,0:T(2,128)(2,1)S(1)} reshape(bf16[4096,128]{1,0:T(8,128)(2,1)} %convolution_convert_fusion.2) | data formatting | bytes 2097152 | tf_op jit(solution)/shard_map/reshape | solution.py:103
  160.7 3.6 copy.62
  166.3 6.7 %convolution_convert_fusion.3 = bf16[4096,128]{1,0:T(8,128)(2,1)} fusion(bf16[4096,1024]{1,0:T(8,128)(2,1)} %bitcast.102, bf16[2,1024,1408]{2,1,0:T(8,128)(2,1)} %all-gather.3.cloned.1.call-done), kind=kOutput, calls=%fused_computation.12 | convolution fusion | flops 1074266112 | bytes 9699328 | tf_op jit(solution)/shard_map/dot_general | solution.py:41
  173.0 4.0 %reshape.1022 = bf16[2,2048,2,64]{3,2,1,0:T(2,128)(2,1)S(1)} reshape(bf16[4096,128]{1,0:T(8,128)(2,1)} %convolution_convert_fusion.3) | data formatting | bytes 2097152 | tf_op jit(solution)/shard_map/reshape | solution.py:110
  177.0 3.5 copy.59
  180.5 2.0 fusion.216
  182.5 2.5 fusion.15
  186.7 3.7 %all-to-all-start.1 = ((bf16[4,128,1024]{2,1,0:T(8,128)(2,1)}), bf16[4,128,1024]{2,1,0:T(8,128)(2,1)S(1)}, u32[]{:S(2)}, u32[]{:S(2)}) async-start(bf16[4,128,1024]{2,1,0:T(8,128)(2,1)} %broadcast_in_dim.13), calls=%async_computation.1 | async-start | bytes 2097152 | tf_op jit(solution)/shard_map/all_to_all | solution.py:26
  190.5 16.1 %all-to-all-done.1 = bf16[4,128,1024]{2,1,0:T(8,128)(2,1)S(1)} async-done(((bf16[4,128,1024]{2,1,0:T(8,128)(2,1)}), bf16[4,128,1024]{2,1,0:T(8,128)(2,1)S(1)}, u32[]{:S(2)}, u32[]{:S(2)}) %all-to-all-start.1) | async-done | bytes 1048608 | tf_op jit(solution)/shard_map/all_to_all | solution.py:26
  207.4 67.2 %all-gather.5.cloned.1.call-done = bf16[2,1024,1024]{1,2,0:T(8,128)(2,1)} async-done(((bf16[2,1024,16]{1,2,0:T(8,128)(2,1)}), bf16[2,1024,1024]{1,2,0:T(8,128)(2,1)}) %all-gather.5.cloned.1.call-update) | async-done | bytes 4194320 | tf_op jit(solution)/shard_map/all_gather | solution.py:75
  274.6 4.4 %fusion.13 = bf16[128,1024]{1,0:T(8,128)(2,1)S(1)} fusion(bf16[2,1024,1024]{1,2,0:T(8,128)(2,1)} %all-gather.5.cloned.1.call-done, bf16[128,1024]{1,0:T(8,128)(2,1)S(1)} %bitcast.117, bf16[2,1024,1408]{2,1,0:T(8,128)(2,1)} %all-gather.3.cloned.1.call-done), kind=kOutput, calls=%fused_computation.31 | convolution fusion | flops 545521664 | bytes 4718592 | tf_op jit(solution)/shard_map/dot_general | solution.py:41
  280.1 4.2 %all-to-all-start.2 = ((bf16[4,128,1024]{2,1,0:T(8,128)(2,1)}), bf16[4,128,1024]{2,1,0:T(8,128)(2,1)}, u32[]{:S(2)}, u32[]{:S(2)}) async-start(bf16[4,128,1024]{2,1,0:T(8,128)(2,1)} %broadcast_in_dim.15), calls=%async_computation.2 | async-start | bytes 2097152 | tf_op jit(solution)/shard_map/all_to_all | solution.py:26
  284.4 6.7 %convolution_convert_fusion = bf16[4096,128]{1,0:T(8,128)(2,1)} fusion(bf16[4096,1024]{1,0:T(8,128)(2,1)} %bitcast.99, bf16[2,1024,1408]{2,1,0:T(8,128)(2,1)} %all-gather.3.cloned.1.call-done), kind=kOutput, calls=%fused_computation.9 | convolution fusion | flops 1074266112 | bytes 9699328 | tf_op jit(solution)/shard_map/dot_general | solution.py:41
  291.1 3.9 %reshape.1025 = bf16[2,2048,2,64]{3,2,1,0:T(2,128)(2,1)S(1)} reshape(bf16[4096,128]{1,0:T(8,128)(2,1)} %convolution_convert_fusion) | data formatting | bytes 2097152 | tf_op jit(solution)/shard_map/reshape | solution.py:103
  295.0 3.6 copy.71
  298.5 6.7 %convolution_convert_fusion.1 = bf16[4096,128]{1,0:T(8,128)(2,1)} fusion(bf16[4096,1024]{1,0:T(8,128)(2,1)} %bitcast.100, bf16[2,1024,1408]{2,1,0:T(8,128)(2,1)} %all-gather.3.cloned.1.call-done), kind=kOutput, calls=%fused_computation.10 | convolution fusion | flops 1074266112 | bytes 9699328 | tf_op jit(solution)/shard_map/dot_general | solution.py:41
  305.2 3.9 %reshape.1024 = bf16[2,2048,2,64]{3,2,1,0:T(2,128)(2,1)S(1)} reshape(bf16[4096,128]{1,0:T(8,128)(2,1)} %convolution_convert_fusion.1) | data formatting | bytes 2097152 | tf_op jit(solution)/shard_map/reshape | solution.py:110
  309.1 3.6 copy.68
  312.7 1.5 convert_reduce_fusion.2
  319.0 2.0 fusion.221
  321.0 2.5 fusion.16
  324.1 17.5 %all_to_all.25 = bf16[4,128,1024]{2,1,0:T(8,128)(2,1)S(1)} all-to-all(bf16[4,128,1024]{2,1,0:T(8,128)(2,1)S(1)} %broadcast_in_dim.16), channel_id=1, replica_groups=mesh['dp'=64,'mp'=4] {'mp'}, dimensions={0} | all-to-all | bytes 2097152 | tf_op jit(solution)/shard_map/all_to_all | solution.py:26
  342.5 4.4 %fusion.14 = bf16[128,1024]{1,0:T(8,128)(2,1)S(1)} fusion(bf16[2,1024,1024]{1,2,0:T(8,128)(2,1)} %all-gather.5.cloned.1.call-done, bf16[128,1024]{1,0:T(8,128)(2,1)S(1)} %bitcast.116, bf16[2,1024,1408]{2,1,0:T(8,128)(2,1)} %all-gather.3.cloned.1.call-done), kind=kOutput, calls=%fused_computation.32 | convolution fusion | flops 545521664 | bytes 4718592 | tf_op jit(solution)/shard_map/dot_general | solution.py:41
  347.0 16.9 %all_to_all.26 = bf16[4,128,1024]{2,1,0:T(8,128)(2,1)S(1)} all-to-all(bf16[4,128,1024]{2,1,0:T(8,128)(2,1)S(1)} %broadcast_in_dim.17), channel_id=1, replica_groups=mesh['dp'=64,'mp'=4] {'mp'}, dimensions={0} | all-to-all | bytes 2097152 | tf_op jit(solution)/shard_map/all_to_all | solution.py:26
  (91 shorter events, 22.7 us)
Async XLA Ops:
  6.5 140.9 %all-gather.3.cloned.1.call-start = ((), (), s32[]{:S(2)}) async-start(), calls=%async_computation.5 | async-start | bytes 5857280 | tf_op jit(solution)/shard_map/all_gather | solution.py:20
  9.6 35.9 %all-to-all-start = ((bf16[64,2,128,16]{2,3,1,0:T(8,128)(2,1)}), bf16[64,2,128,16]{2,3,1,0:T(8,128)(2,1)S(1)}, u32[]{:S(2)}, u32[]{:S(2)}) async-start(bf16[64,2,128,16]{2,3,1,0:T(8,128)(2,1)} %stack.2), calls=%async_computation | async-start | bytes 1048576 | tf_op jit(solution)/shard_map/all_to_all | solution.py:13
  23.8 250.8 %all-gather.5.cloned.1.call-start = ((), (), s32[]{:S(2)}) async-start(), calls=%async_computation.6 | async-start | bytes 4259840 | tf_op jit(solution)/shard_map/all_gather | solution.py:75
  29.1 5.8 %copy-start = (bf16[2,8,256,1024]{3,2,1,0:T(8,128)(2,1)S(1)}, bf16[2,8,256,1024]{3,2,1,0:T(8,128)(2,1)}, u32[]{:S(2)}) copy-start(bf16[2,8,256,1024]{3,2,1,0:T(8,128)(2,1)} %param.13) | copy-start | bytes 25165828
  173.0 7.5 %copy-start.2 = (bf16[2,2048,2,64]{1,3,2,0:T(8,128)(2,1)S(1)}, bf16[2,2048,2,64]{1,3,2,0:T(8,128)(2,1)}, u32[]{:S(2)}) copy-start(bf16[2,2048,2,64]{1,3,2,0:T(8,128)(2,1)} %copy.62) | copy-start | bytes 3145732
  182.5 2.8 copy-start.4
  185.1 5.4 %copy-start.5 = (f32[2,1024]{1,0:T(2,128)S(1)}, f32[2,1024]{1,0:T(2,128)}, u32[]{:S(2)}) copy-start(f32[2,1024]{1,0:T(2,128)} %param.18) | copy-start | bytes 24580
  186.7 19.9 %all-to-all-start.1 = ((bf16[4,128,1024]{2,1,0:T(8,128)(2,1)}), bf16[4,128,1024]{2,1,0:T(8,128)(2,1)S(1)}, u32[]{:S(2)}, u32[]{:S(2)}) async-start(bf16[4,128,1024]{2,1,0:T(8,128)(2,1)} %broadcast_in_dim.13), calls=%async_computation.1 | async-start | bytes 2097152 | tf_op jit(solution)/shard_map/all_to_all | solution.py:26
  280.1 32.6 %all-to-all-start.2 = ((bf16[4,128,1024]{2,1,0:T(8,128)(2,1)}), bf16[4,128,1024]{2,1,0:T(8,128)(2,1)}, u32[]{:S(2)}, u32[]{:S(2)}) async-start(bf16[4,128,1024]{2,1,0:T(8,128)(2,1)} %broadcast_in_dim.15), calls=%async_computation.2 | async-start | bytes 2097152 | tf_op jit(solution)/shard_map/all_to_all | solution.py:26
  312.7 6.3 %copy-start.1 = (bf16[2,2048,2,64]{1,3,2,0:T(8,128)(2,1)S(1)}, bf16[2,2048,2,64]{1,3,2,0:T(8,128)(2,1)}, u32[]{:S(2)}) copy-start(bf16[2,2048,2,64]{1,3,2,0:T(8,128)(2,1)} %copy.71) | copy-start | bytes 3145732
  321.0 2.7 copy-start.3
  346.8 17.7 %copy-start.6 = (f32[1024]{0:T(1024)S(1)}, f32[1024]{0:T(1024)}, u32[]{:S(2)}) copy-start(f32[1024]{0:T(1024)} %param.19) | copy-start | bytes 12292
Sparse Core Ops, SparseCore 0:
  11.0 136.4 all-gather.2
  151.0 123.5 all-gather.4
